TPU v7x, 32 devices: a whole 2x2x4 slice. The times are simulated.
32 devices in a mesh: group: 2 (over y), batch: 4 (over z), expert: 4 (over x, core).
Axes of the slice: x: 2, y: 2, z: 4, core: 2. Of those that a mesh axis runs over, the one named last changes fastest.
Arguments:
- residual_in: bfloat16 [128, 4096], P(('group', 'batch')), parts along dimension 0, may hold values from -11 to 11
- queries: bfloat16 [128, 16, 128], P(('group', 'batch'), 'expert'), parts along dimension 0, may hold values from -150 to 150
- key_new: bfloat16 [128, 4, 128], P(('group', 'batch'), 'expert'), parts along dimension 0, may hold values from -6 to 6
- value_new: bfloat16 [128, 4, 128], P(('group', 'batch'), 'expert'), parts along dimension 0, may hold values from -6 to 6
- key_cache: bfloat16 [128, 4, 256, 128], P(('group', 'batch'), 'expert'), parts along dimension 0, may hold values from -6 to 6
- value_cache: bfloat16 [128, 4, 256, 128], P(('group', 'batch'), 'expert'), parts along dimension 0, may hold values from -6 to 6
- cache_len: int32 [128], P(('group', 'batch')), parts along dimension 0, may hold values from 1 to 256, 8192 in all
- new_slot: int32 [128], P(('group', 'batch')), parts along dimension 0, may hold values 0 or 1
- out_weight: bfloat16 [2048, 4096], P('expert'), may hold values from -0.125 to 0.125
- norm_gain: float32 [4096], replicated, may hold values from 0.5 to 1.5
- router: bfloat16 [4096, 4], replicated, may hold values from -0.09375 to 0.09375
- chosen: int32 [128, 2], P(('group', 'batch')), parts along dimension 0, may hold values from 0 to 3, all different within a row; in each aligned block of 16 rows (0 to 15, 16 to 31, ...) at most 12 rows name the same one
- w_gate: bfloat16 [4, 4096, 8192], P('expert', None, 'batch'), may hold values from -0.09375 to 0.09375
- w_up: bfloat16 [4, 4096, 8192], P('expert', None, 'batch'), may hold values from -0.09375 to 0.09375
- w_down: bfloat16 [4, 8192, 4096], P('expert', 'batch'), may hold values from -0.0625 to 0.0625
Outputs:
- layer_out: bfloat16 [128, 4096], P(('group', 'batch', 'expert')), parts along dimension 0
There are 2 independent parts, one for each index of `group`. A program takes and returns all parts, laid end to end along the dimension named above; an argument that names none is the same for every part. Nothing has to cross between parts.
Inputs may be any that keep to these rules, and one draw needn't show every extreme that they name: `chosen`: each row names 2 different experts. Among the rows of one device no expert is named by more than 12 rows, and in every draw some expert is named by exactly 12 rows of some device. `cache_len`: the lengths of a part sum to 8192, and the largest is exactly 256.
All inputs are finite; a program needn't handle non-finite values. No bound on the sum of `cache_len` or of `new_slot` on one device may be relied on, other than what follows from the above.
Results may differ from a plain program's by a relative error of at most 0.017.
Values may be sent and summed in bfloat16 or wider, within the bound.
No kernel may reach another device: no remote copies, remote signals or barrier semaphores. Data moves between devices by JAX's collectives and lax.ppermute only.
A program may use at most 128 MiB of HBM per device.

v0:
```python
import jax
import jax.numpy as jnp
from jax import lax
from jax.sharding import PartitionSpec as P

CAP = 12
epsilon = 1e-05


def attend(queries, key_new, value_new, key_cache, value_cache, cache_len, new_slot):
    slot_count, kv_count, length, head_width = key_cache.shape
    group_size = queries.shape[1] // kv_count
    grouped = queries.reshape(slot_count, kv_count, group_size, head_width)
    scaling = float(head_width) ** (-0.5)
    scores = (
        jnp.einsum("skgd,sktd->skgt", grouped, key_cache, preferred_element_type=jnp.float32)
        * scaling
    )
    own_score = (
        jnp.einsum("skgd,skd->skg", grouped, key_new, preferred_element_type=jnp.float32) * scaling
    )
    places = lax.broadcasted_iota(jnp.int32, (slot_count, length), 1)
    usable = (places < cache_len[:, None]) & (new_slot[:, None] == 0)
    usable = usable[:, None, None, :]
    scores = jnp.where(usable, scores, jnp.float32(-1e30))
    highest = jnp.maximum(jnp.max(scores, axis=3), own_score)
    weights = jnp.where(usable, jnp.exp(scores - highest[..., None]), jnp.float32(0.0))
    own_weight = jnp.exp(own_score - highest)
    denominator = jnp.sum(weights, axis=3) + own_weight
    probabilities = (weights / denominator[..., None]).astype(jnp.bfloat16)
    own_prob = (own_weight / denominator).astype(jnp.bfloat16)
    attended = jnp.einsum(
        "skgt,sktd->skgd", probabilities, value_cache, preferred_element_type=jnp.float32
    )
    attended = (
        attended
        + own_prob.astype(jnp.float32)[..., None] * value_new.astype(jnp.float32)[:, :, None, :]
    )
    return attended.reshape(slot_count, kv_count * group_size * head_width).astype(jnp.bfloat16)


def mixing(logits, chosen, expert_count):
    labels = lax.broadcasted_iota(jnp.int32, (1, 1, expert_count), 2)
    picking = (chosen[:, :, None] == labels).astype(jnp.float32)
    chosen_logits = jnp.sum(picking * logits[:, None, :], axis=2)
    leading = jax.nn.sigmoid(chosen_logits[:, 0] - chosen_logits[:, 1])
    fractions = jnp.stack([leading, 1.0 - leading], axis=1)
    return jnp.sum(picking * fractions[:, :, None], axis=1)


def placement_table(chosen, targets, capacity):
    routed = jnp.sum((chosen[None, :, :] == targets[:, None, None]).astype(jnp.int32), axis=2)
    position = jnp.cumsum(routed, axis=1) - routed
    row_labels = lax.broadcasted_iota(jnp.int32, (1, capacity, 1), 1)
    return ((position[:, None, :] == row_labels) & (routed[:, None, :] == 1)).astype(jnp.float32)


def body(
    residual_in,
    queries,
    key_new,
    value_new,
    key_cache,
    value_cache,
    cache_len,
    new_slot,
    out_weight,
    norm_gain,
    router,
    chosen,
    w_gate,
    w_up,
    w_down,
):
    my_expert = lax.axis_index("expert")
    attended = attend(queries, key_new, value_new, key_cache, value_cache, cache_len, new_slot)
    partial_value = jnp.dot(attended, out_weight, preferred_element_type=jnp.float32)
    summed = lax.psum(partial_value, "expert")
    stream = (residual_in.astype(jnp.float32) + summed).astype(jnp.bfloat16)
    values = stream.astype(jnp.float32)
    scaling = lax.rsqrt(jnp.mean(values * values, axis=1, keepdims=True) + epsilon)
    normed = (values * scaling * norm_gain).astype(jnp.bfloat16)
    logits = jnp.dot(normed, router, preferred_element_type=jnp.float32)
    placing = placement_table(chosen, jnp.reshape(my_expert, (1,)), CAP)[0]
    sent_rows = jnp.dot(
        placing.astype(jnp.bfloat16), normed, preferred_element_type=jnp.float32
    ).astype(jnp.bfloat16)
    carried = values * (my_expert == 0).astype(jnp.float32)
    coef = mixing(logits, chosen, router.shape[1])
    expert_labels = lax.broadcasted_iota(jnp.int32, (1, router.shape[1]), 1)
    my_coef = jnp.sum(coef * (expert_labels == my_expert).astype(jnp.float32), axis=1)
    row_weight = jnp.dot(placing, my_coef, precision=lax.Precision.HIGHEST)
    block_rows = lax.all_gather(sent_rows, "batch", axis=0, tiled=True)
    gate_part = jnp.dot(block_rows, w_gate[0], preferred_element_type=jnp.float32)
    up_part = jnp.dot(block_rows, w_up[0], preferred_element_type=jnp.float32)
    hidden = (jax.nn.silu(gate_part) * up_part).astype(jnp.bfloat16)
    block_rows = hidden
    outputs = lax.psum_scatter(
        jnp.dot(block_rows, w_down[0], preferred_element_type=jnp.float32).astype(jnp.bfloat16),
        "batch",
        scatter_dimension=0,
        tiled=True,
    ).astype(jnp.float32)
    weighted = row_weight[:, None] * outputs
    contribution = jnp.dot(placing.T, weighted, precision=lax.Precision.HIGHEST) + carried
    layer_out = lax.psum_scatter(
        contribution.astype(jnp.bfloat16), "expert", scatter_dimension=0, tiled=True
    )
    return layer_out


def solution(mesh):
    in_specs = (
        P(("group", "batch"), None),
        P(("group", "batch"), "expert", None),
        P(("group", "batch"), "expert", None),
        P(("group", "batch"), "expert", None),
        P(("group", "batch"), "expert", None, None),
        P(("group", "batch"), "expert", None, None),
        P(("group", "batch")),
        P(("group", "batch")),
        P("expert", None),
        P(),
        P(),
        P(("group", "batch"), None),
        P("expert", None, "batch"),
        P("expert", None, "batch"),
        P("expert", "batch", None),
    )
    out_specs = P(("group", "batch", "expert"), None)
    return jax.shard_map(body, mesh=mesh, in_specs=in_specs, out_specs=out_specs, check_vma=False)
```

profile of v0, /device:TPU:0, one launch (start us, length us, event | category | flops | bytes accessed | tf_op | source)
XLA Modules:
  0.0 154.4 jit_solution(7242869067965577408)
XLA Ops:
  6.5 0.0 copy-start
  6.5 0.0 all-reduce.6.cloned.1.call-start
  6.5 0.7 broadcast_compare_fusion
  7.3 0.7 fusion.48
  8.0 0.9 fusion.52
  8.9 0.0 copy-done
  8.9 1.2 fusion.67
  10.1 0.2 fusion.37
  10.3 0.7 bitcast_convert_fusion
  11.0 1.5 fusion.19
  12.5 3.6 %fusion.45 = f32[16,4096]{1,0:T(8,128)} fusion(bf16[512,4096]{1,0:T(8,128)(2,1)} %param.23, bf16[2,8,4,128]{3,2,1,0:T(4,128)(2,1)S(1)} %bitcast.56), kind=kOutput, calls=%fused_computation.45 | convolution fusion | flops 67108864 | bytes 4472832 | tf_op jit(solution)/shard_map/dot_general | solution.py:77
  16.1 0.0 all-reduce.6.cloned.1.call-update
  16.1 0.0 all-reduce.8.cloned.1.call-start
  16.1 0.7 fusion.63
  16.8 0.1 copy.26
  17.0 0.1 reduce.6
  17.1 1.2 dynamic-slice.6
  19.0 32.2 %all-reduce.6.cloned.1.call-done = f32[16,4096]{1,0:T(8,128)} async-done(((f32[16,4096]{1,0:T(8,128)}), f32[16,4096]{1,0:T(8,128)}) %all-reduce.6.cloned.1.call-update) | async-done | bytes 262160 | tf_op jit(solution)/shard_map/psum | solution.py:78
  51.2 1.1 fusion.29
  52.4 1.0 fusion.11
  53.3 15.2 %all-gather = bf16[4,12,4096]{2,1,0:T(8,128)(2,1)S(1)} all-gather(bf16[1,12,4096]{2,1,0:T(8,128)(2,1)S(1)} %fusion.11), channel_id=1, replica_groups=mesh['group'=2,'batch'=4,'expert'=4] {'batch'}, dimensions={0}, use_global_device_ids=true | all-gather | bytes 491520 | tf_op jit(solution)/shard_map/all_gather | solution.py:93
  68.5 0.1 reshape.221
  68.6 8.8 %fusion.5 = f32[48,2048]{1,0:T(8,128)S(1)} fusion(bf16[48,4096]{1,0:T(8,128)(2,1)S(1)} %reshape.221, bf16[1,4096,2048]{2,1,0:T(8,128)(2,1)} %param.27), kind=kOutput, calls=%fused_computation.4 | convolution fusion | flops 805306368 | bytes 17563648 | tf_op jit(solution)/shard_map/dot_general | solution.py:94
  77.4 0.0 copy-start.1
  77.4 0.0 copy-start.3
  77.4 0.0 copy-start.2
  77.4 0.0 copy-start.4
  77.5 13.7 %fusion.7 = bf16[48,4096]{1,0:T(8,128)(2,1)S(1)} fusion(bf16[1,2048,4096]{2,1,0:T(8,128)(2,1)} %param.29, bf16[48,4096]{1,0:T(8,128)(2,1)S(1)} %reshape.221, bf16[1,4096,2048]{2,1,0:T(8,128)(2,1)} %param.28, f32[48,2048]{1,0:T(8,128)S(1)} %fusion.5), kind=kOutput, calls=%fused_computation.6 | convolution fusion | flops 1611399168 | bytes 34734080 | tf_op jit(solution)/shard_map/dot_general | solution.py:99
  91.1 16.0 %fusion = bf16[16,4096]{1,0:T(8,128)(2,1)S(1)} fusion(bf16[48,4096]{1,0:T(8,128)(2,1)S(1)} %fusion.7), kind=kCustom, calls=%all-reduce-scatter | all-reduce-scatter fusion | flops 262145 | bytes 524800
  107.2 2.8 %collective-permute-start = (bf16[12,4096]{1,0:T(8,128)(2,1)S(1)}, bf16[12,4096]{1,0:T(8,128)(2,1)S(1)}, u32[]{:S(2)}, u32[]{:S(2)}) collective-permute-start(bf16[12,4096]{1,0:T(8,128)(2,1)S(1)} %slice.8), channel_id=1, source_target_pairs={{0,4},{4,8},{8,12},{1,5},{5,9},{9,13},{2,6},{6,10},{10,14},{3,7},{... | collective-permute-start | bytes 294920
  110.0 0.0 copy-done.1
  110.1 0.0 copy-done.3
  110.1 0.2 fusion.43
  110.3 0.0 copy-done.2
  110.4 0.1 multiply_reduce_fusion
  110.5 0.1 convolution_bitcast_fusion
  110.6 2.0 %collective-permute-done = bf16[12,4096]{1,0:T(8,128)(2,1)S(1)} collective-permute-done((bf16[12,4096]{1,0:T(8,128)(2,1)S(1)}, bf16[12,4096]{1,0:T(8,128)(2,1)S(1)}, u32[]{:S(2)}, u32[]{:S(2)}) %collective-permute-start) | collective-permute-done | bytes 98336
  112.5 0.3 concatenate
  112.9 1.0 fusion.10
  113.9 0.0 all-reduce.8.cloned.1.call-update
  113.9 0.0 copy-done.4
  113.9 0.6 dynamic-slice.2
  115.1 31.0 %all-reduce.8.cloned.1.call-done = bf16[16,4096]{1,0:T(8,128)(2,1)} async-done(((bf16[16,4096]{1,0:T(8,128)(2,1)}), bf16[16,4096]{1,0:T(8,128)(2,1)}) %all-reduce.8.cloned.1.call-update) | async-done | bytes 131088
  146.1 1.5 constant_dynamic-slice_fusion
  (12 shorter events, 0.2 us)
Async XLA Ops:
  6.5 2.3 %copy-start = (bf16[16,1,256,128]{3,2,1,0:T(8,128)(2,1)S(1)}, bf16[16,1,256,128]{3,2,1,0:T(8,128)(2,1)}, u32[]{:S(2)}) copy-start(bf16[16,1,256,128]{3,2,1,0:T(8,128)(2,1)} %param.19) | copy-start | bytes 3145732
  6.5 44.7 %all-reduce.6.cloned.1.call-start = ((), (), s32[]{:S(2)}) async-start(), calls=%async_computation | async-start | bytes 524288 | tf_op jit(solution)/shard_map/psum | solution.py:78
  16.1 130.0 %all-reduce.8.cloned.1.call-start = ((), (), s32[]{:S(2)}) async-start(), calls=%async_computation.1 | async-start | bytes 262144
  77.4 32.6 %copy-start.1 = (f32[4096]{0:T(1024)S(1)}, f32[4096]{0:T(1024)}, u32[]{:S(2)}) copy-start(f32[4096]{0:T(1024)} %param.24) | copy-start | bytes 49156
  77.4 32.6 %copy-start.3 = (bf16[4096,4]{0,1:T(4,128)(2,1)S(1)}, bf16[4096,4]{0,1:T(4,128)(2,1)}, u32[]{:S(2)}) copy-start(bf16[4096,4]{0,1:T(4,128)(2,1)} %param.25) | copy-start | bytes 98308
  77.4 32.9 %copy-start.2 = (s32[16,2]{0,1:T(2,128)S(1)}, s32[16,2]{0,1:T(2,128)}, u32[]{:S(2)}) copy-start(s32[16,2]{0,1:T(2,128)} %param.26) | copy-start | bytes 388
  77.4 36.4 %copy-start.4 = (u32[32]{0:T(128)S(1)}, u32[32]{0:T(128)}, u32[]{:S(2)}) copy-start(u32[32]{0:T(128)} %constant.45) | copy-start | bytes 388
  107.2 5.4 %collective-permute-start = (bf16[12,4096]{1,0:T(8,128)(2,1)S(1)}, bf16[12,4096]{1,0:T(8,128)(2,1)S(1)}, u32[]{:S(2)}, u32[]{:S(2)}) collective-permute-start(bf16[12,4096]{1,0:T(8,128)(2,1)S(1)} %slice.8), channel_id=1, source_target_pairs={{0,4},{4,8},{8,12},{1,5},{5,9},{9,13},{2,6},{6,10},{10,14},{3,7},{... | collective-permute-start | bytes 294920
Sparse Core Ops, SparseCore 0:
  16.2 34.9 all-reduce.5
  114.0 32.0 all-reduce.7
where the time goes:
time: 155 us; the launch traced here: 154 us
  waiting for transfers between devices  65.2 us (42%)
  matrix products  31.9 us (21%)
  blocking collectives  31.2 us (20%)
  between operations  14.9 us (10%)
  other arithmetic  4.53 us (3%)
  local copies, waits for them, and re-layouts  3.85 us (2%)
  starting transfers between devices  2.89 us (2%)
    unnamed x4, waiting for transfers between devices  33 us
    psum x1, waiting for transfers between devices, body(): summed = lax.psum(partial_value, 'expert')  32.2 us
    unnamed x1, blocking collectives  16 us
    all_gather x1, blocking collectives, body(): block_rows = lax.all_gather(sent_rows, 'batch', axis=0, tiled=True)  15.2 us
    dot_general x1, matrix products, body(): jnp.dot(block_rows, w_down[0], preferred_element_type=jnp.float32)  13.7 us
    dot_general x1, matrix products, body(): jnp.dot(block_rows, w_gate[0], preferred_element_type=jnp.float32)  8.79 us
    unnamed x16, local copies, waits for them, and re-layouts  3.76 us
    dot_general x1, matrix products, body(): jnp.dot(attended, out_weight, preferred_element_type=jnp.float32)  3.56 us
  transfers between devices with their start and end apart: 3, of which 3 were waited for; matrix products, arithmetic and copies ran while one was open for 2% of the time, Pallas kernels for 0%

commit v1 on v0

--- a/solution.py
+++ b/solution.py
@@ -5,6 +5,14 @@
 
 CAP = 12
 epsilon = 1e-05
+
+
+def doubling_sum(x, name):
+    peers, total = (lax.axis_size(name), x)
+    for far in [1 << k for k in range(peers.bit_length() - 1)]:
+        route = [(i, i ^ far) for i in range(peers)]
+        total = total + lax.ppermute(total, name, route)
+    return total
 
 
 def attend(queries, key_new, value_new, key_cache, value_cache, cache_len, new_slot):
@@ -75,7 +83,7 @@
     my_expert = lax.axis_index("expert")
     attended = attend(queries, key_new, value_new, key_cache, value_cache, cache_len, new_slot)
     partial_value = jnp.dot(attended, out_weight, preferred_element_type=jnp.float32)
-    summed = lax.psum(partial_value, "expert")
+    summed = doubling_sum(partial_value, "expert")
     stream = (residual_in.astype(jnp.float32) + summed).astype(jnp.bfloat16)
     values = stream.astype(jnp.float32)
     scaling = lax.rsqrt(jnp.mean(values * values, axis=1, keepdims=True) + epsilon)

time: 155 us -> 134 us (0.86)
  waiting for transfers between devices: 65.2 us -> 38.6 us
  starting transfers between devices: 2.89 us -> 5.87 us
  blocking collectives: 31.2 us -> 32.8 us
    psum x1 -> x0, waiting for transfers between devices: 32.2 us -> none  [body(): summed = lax.psum(partial_value, 'expert')]
    ppermute x0 -> x2, waiting for transfers between devices: none -> 4.91 us  [doubling_sum(): total = total + lax.ppermute(total, name, route)]
    ppermute x0 -> x2, starting transfers between devices: none -> 3.41 us  [doubling_sum(): total = total + lax.ppermute(total, name, route)]
    unnamed x4 -> x3, waiting for transfers between devices: 33 us -> 33.7 us
    unnamed x16 -> x10, local copies, waits for them, and re-layouts: 3.76 us -> 3.74 us
  transfers between devices with their start and end apart: 3 -> 4, of which waited for: 3 -> 4; matrix products, arithmetic and copies ran while one was open for 2% -> 2% of each run, Pallas kernels for 0% -> 0%
where the time goes in v1:
time: 134 us
  waiting for transfers between devices  38.6 us (29%)
  blocking collectives  32.8 us (24%)
  matrix products  31.9 us (24%)
  between operations  14.8 us (11%)
  starting transfers between devices  5.87 us (4%)
  other arithmetic  5.86 us (4%)
  local copies, waits for them, and re-layouts  3.83 us (3%)
    unnamed x3, waiting for transfers between devices  33.7 us
    unnamed x1, blocking collectives  17.1 us
    all_gather x1, blocking collectives, body(): block_rows = lax.all_gather(sent_rows, 'batch', axis=0, tiled=True)  15.7 us
    dot_general x1, matrix products, body(): jnp.dot(block_rows, w_down[0], preferred_element_type=jnp.float32)  13.7 us
    dot_general x1, matrix products, body(): jnp.dot(block_rows, w_gate[0], preferred_element_type=jnp.float32)  8.79 us
    ppermute x2, waiting for transfers between devices, doubling_sum(): total = total + lax.ppermute(total, name, route)  4.91 us
    unnamed x10, local copies, waits for them, and re-layouts  3.74 us
    ppermute x2, starting transfers between devices, doubling_sum(): total = total + lax.ppermute(total, name, route)  3.41 us
  transfers between devices with their start and end apart: 4, of which 4 were waited for; matrix products, arithmetic and copies ran while one was open for 2% of the time, Pallas kernels for 0%

profile of v1, /device:TPU:0, one launch (start us, length us, event | category | flops | bytes accessed | tf_op | source)
XLA Modules:
  0.0 133.6 jit_solution(3723533601127072040)
XLA Ops:
  6.5 0.0 copy-start
  6.5 0.0 all-reduce.5.cloned.1.call-start
  6.5 0.7 broadcast_compare_fusion
  7.3 0.7 fusion.48
  8.0 0.9 fusion.52
  8.9 0.0 copy-done
  8.9 1.2 fusion.67
  10.1 0.2 fusion.37
  10.3 0.7 bitcast_convert_fusion
  11.0 1.5 %fusion.19 = bf16[16,4,128]{2,1,0:T(4,128)(2,1)S(1)} fusion(bf16[16,1,256,128]{3,2,1,0:T(8,128)(2,1)} %param.20, f32[16,4,256]{2,1,0:T(4,128)S(1)} %get-tuple-element.12, f32[16,4]{1,0:T(8,128)S(1)} %get-tuple-element.10, f32[16,4]{1,0:T(8,128)S(1)} %multiply_maximum_fusion, pred[16,256]{1,0:T(8,128)(4,1)S(1)} %fusion.48, ...), kind=kOutput, calls=%fused_computation.16 | convolution fusion | flops 4284416 | bytes 1143552 | tf_op jit(solution)/shard_map/skgt,sktd->skgd/dot_general | solution.py:40
  12.5 2.9 %fusion.45 = f32[16,4096]{1,0:T(8,128)S(1)} fusion(bf16[512,4096]{1,0:T(8,128)(2,1)} %param.23, bf16[2,8,4,128]{3,2,1,0:T(4,128)(2,1)S(1)} %bitcast.56), kind=kOutput, calls=%fused_computation.45 | convolution fusion | flops 67108864 | bytes 4472832 | tf_op jit(solution)/shard_map/dot_general | solution.py:85
  15.4 0.5 collective-permute-start
  15.9 0.7 fusion.63
  16.6 0.5 collective-permute-done
  17.1 2.9 %collective-permute-start.1 = (f32[16,4096]{1,0:T(8,128)S(1)}, f32[16,4096]{1,0:T(8,128)S(1)}, u32[]{:S(2)}, u32[]{:S(2)}) collective-permute-start(f32[16,4096]{1,0:T(8,128)S(1)} %add.43), channel_id=1, source_target_pairs={{0,2},{1,3},{2,0},{3,1},{4,6},{5,7},{6,4},{7,5},{8,10},{9,11},{10,... | collective-permute-start | bytes 786440 | tf_op jit(solution)/shard_map/ppermute | solution.py:14
  20.0 0.1 copy.26
  20.1 0.1 reduce.6
  20.2 1.2 dynamic-slice.6
  22.1 4.4 %collective-permute-done.1 = f32[16,4096]{1,0:T(8,128)S(1)} collective-permute-done((f32[16,4096]{1,0:T(8,128)S(1)}, f32[16,4096]{1,0:T(8,128)S(1)}, u32[]{:S(2)}, u32[]{:S(2)}) %collective-permute-start.1) | collective-permute-done | bytes 262176 | tf_op jit(solution)/shard_map/ppermute | solution.py:14
  26.6 1.1 fusion.29
  27.6 1.0 fusion.43
  28.6 0.7 select_reduce_fusion.1
  29.4 0.7 select_reduce_fusion
  30.1 0.9 fusion.11
  31.0 15.7 %all-gather = bf16[4,12,4096]{2,1,0:T(8,128)(2,1)S(1)} all-gather(bf16[1,12,4096]{2,1,0:T(8,128)(2,1)S(1)} %fusion.11), channel_id=1, replica_groups=mesh['group'=2,'batch'=4,'expert'=4] {'batch'}, dimensions={0}, use_global_device_ids=true | all-gather | bytes 491520 | tf_op jit(solution)/shard_map/all_gather | solution.py:101
  46.7 0.1 reshape.221
  46.8 8.8 %fusion.5 = f32[48,2048]{1,0:T(8,128)S(1)} fusion(bf16[48,4096]{1,0:T(8,128)(2,1)S(1)} %reshape.221, bf16[1,4096,2048]{2,1,0:T(8,128)(2,1)} %param.27), kind=kOutput, calls=%fused_computation.4 | convolution fusion | flops 805306368 | bytes 17563648 | tf_op jit(solution)/shard_map/dot_general | solution.py:102
  55.6 0.0 copy-start.1
  55.6 13.7 %fusion.7 = bf16[48,4096]{1,0:T(8,128)(2,1)S(1)} fusion(bf16[1,2048,4096]{2,1,0:T(8,128)(2,1)} %param.29, bf16[48,4096]{1,0:T(8,128)(2,1)S(1)} %reshape.221, bf16[1,4096,2048]{2,1,0:T(8,128)(2,1)} %param.28, f32[48,2048]{1,0:T(8,128)S(1)} %fusion.5), kind=kOutput, calls=%fused_computation.6 | convolution fusion | flops 1611399168 | bytes 34734080 | tf_op jit(solution)/shard_map/dot_general | solution.py:107
  69.3 17.1 %fusion = bf16[16,4096]{1,0:T(8,128)(2,1)S(1)} fusion(bf16[48,4096]{1,0:T(8,128)(2,1)S(1)} %fusion.7), kind=kCustom, calls=%all-reduce-scatter | all-reduce-scatter fusion | flops 262145 | bytes 524800
  86.4 2.5 %collective-permute-start.2 = (bf16[12,4096]{1,0:T(8,128)(2,1)S(1)}, bf16[12,4096]{1,0:T(8,128)(2,1)S(1)}, u32[]{:S(2)}, u32[]{:S(2)}) collective-permute-start(bf16[12,4096]{1,0:T(8,128)(2,1)S(1)} %slice.8), channel_id=1, source_target_pairs={{0,4},{4,8},{8,12},{1,5},{5,9},{9,13},{2,6},{6,10},{10,14},{3,7},{... | collective-permute-start | bytes 294920
  88.9 0.1 multiply_reduce_fusion
  89.0 0.1 convolution_bitcast_fusion
  89.1 2.3 %collective-permute-done.2 = bf16[12,4096]{1,0:T(8,128)(2,1)S(1)} collective-permute-done((bf16[12,4096]{1,0:T(8,128)(2,1)S(1)}, bf16[12,4096]{1,0:T(8,128)(2,1)S(1)}, u32[]{:S(2)}, u32[]{:S(2)}) %collective-permute-start.2) | collective-permute-done | bytes 98336
  91.4 0.3 concatenate
  91.7 1.0 fusion.10
  92.7 0.0 all-reduce.5.cloned.1.call-update
  92.7 0.0 copy-done.1
  92.7 0.6 dynamic-slice.2
  94.0 31.3 %all-reduce.5.cloned.1.call-done = bf16[16,4096]{1,0:T(8,128)(2,1)} async-done(((bf16[16,4096]{1,0:T(8,128)(2,1)}), bf16[16,4096]{1,0:T(8,128)(2,1)}) %all-reduce.5.cloned.1.call-update) | async-done | bytes 131088
  125.3 1.5 %constant_dynamic-slice_fusion = bf16[4,4096]{1,0:T(4,128)(2,1)} fusion(bf16[16,4096]{1,0:T(8,128)(2,1)} %all-reduce.5.cloned.1.call-done, u32[]{:T(128)S(6)} %multiply.9), kind=kLoop, calls=%fused_computation.76 | loop fusion | bytes 65540
  (11 shorter events, 0.2 us)
Async XLA Ops:
  6.5 2.3 %copy-start = (bf16[16,1,256,128]{3,2,1,0:T(8,128)(2,1)S(1)}, bf16[16,1,256,128]{3,2,1,0:T(8,128)(2,1)}, u32[]{:S(2)}) copy-start(bf16[16,1,256,128]{3,2,1,0:T(8,128)(2,1)} %param.19) | copy-start | bytes 3145732
  6.5 118.8 %all-reduce.5.cloned.1.call-start = ((), (), s32[]{:S(2)}) async-start(), calls=%async_computation | async-start | bytes 262144
  15.4 1.7 %collective-permute-start = (f32[16,4096]{1,0:T(8,128)S(1)}, f32[16,4096]{1,0:T(8,128)S(1)}, u32[]{:S(2)}, u32[]{:S(2)}) collective-permute-start(f32[16,4096]{1,0:T(8,128)S(1)} %fusion.45), channel_id=1, source_target_pairs={{0,1},{1,0},{2,3},{3,2},{4,5},{5,4},{6,7},{7,6},{8,9},{9,8},{10,11... | collective-permute-start | bytes 786440 | tf_op jit(solution)/shard_map/ppermute | solution.py:14
  17.1 9.5 %collective-permute-start.1 = (f32[16,4096]{1,0:T(8,128)S(1)}, f32[16,4096]{1,0:T(8,128)S(1)}, u32[]{:S(2)}, u32[]{:S(2)}) collective-permute-start(f32[16,4096]{1,0:T(8,128)S(1)} %add.43), channel_id=1, source_target_pairs={{0,2},{1,3},{2,0},{3,1},{4,6},{5,7},{6,4},{7,5},{8,10},{9,11},{10,... | collective-permute-start | bytes 786440 | tf_op jit(solution)/shard_map/ppermute | solution.py:14
  55.6 37.1 %copy-start.1 = (u32[32]{0:T(128)S(1)}, u32[32]{0:T(128)}, u32[]{:S(2)}) copy-start(u32[32]{0:T(128)} %constant.45) | copy-start | bytes 388
  86.4 5.0 %collective-permute-start.2 = (bf16[12,4096]{1,0:T(8,128)(2,1)S(1)}, bf16[12,4096]{1,0:T(8,128)(2,1)S(1)}, u32[]{:S(2)}, u32[]{:S(2)}) collective-permute-start(bf16[12,4096]{1,0:T(8,128)(2,1)S(1)} %slice.8), channel_id=1, source_target_pairs={{0,4},{4,8},{8,12},{1,5},{5,9},{9,13},{2,6},{6,10},{10,14},{3,7},{... | collective-permute-start | bytes 294920
Sparse Core Ops, SparseCore 0:
  92.8 32.4 all-reduce.4
